TPU v7x, 256 devices: a whole 4x4x8 slice. The times are simulated.
256 devices in a mesh: lvl: 16 (over y_hi, z), lon: 16 (over x, y_lo, core).
Axes of the slice: x: 4, y: 4 (y_hi: 2, y_lo: 2; y = y_hi * 2 + y_lo), z: 8, core: 2. Of those that a mesh axis runs over, the one named last changes fastest.
Arguments:
- window: float32 [16, 16, 69, 2048], P('lvl', None, None, 'lon'), may hold values from -6 to 6
- anchor: float32 [16, 69, 2048], P(None, None, 'lon'), may hold values from -6 to 6
- noise: float32 [16, 16, 69, 2048], P('lvl', None, None, 'lon'), may hold values from -6 to 6
- conv_in: bfloat16 [3, 3, 192, 69], replicated, may hold values from -0.25 to 0.25
- conv_out: bfloat16 [3, 3, 69, 192], replicated, may hold values from -0.15625 to 0.15625
- time_shift: float32 [192], replicated, may hold values from -4 to 4
- plan: int32 [256], replicated, may hold values from 0 to 999, as said below
- start: int32 [1], replicated, may hold values from 0 to 239
Outputs:
- advanced: float32 [16, 16, 69, 2048], P('lvl', None, None, 'lon')
Inputs may be any that keep to these rules, and one draw needn't show every extreme that they name: `plan`: strictly decreasing, first entry 999.
All inputs are finite; a program needn't handle non-finite values.
Results may differ from a plain program's by a relative error of at most 0.0003.
Values may be sent and summed in bfloat16 or wider, within the bound.
A program may use at most 64 MiB of HBM per device.

v0:
```python
import jax
import jax.numpy as jnp
from jax import lax
from jax.sharding import PartitionSpec as P

SWEEPS = 2


def extended(block, sides, width):
    for axis, dim in sides:
        count = lax.axis_size(axis)
        forward = [(i, i + 1) for i in range(count - 1)]
        forward.append((count - 1, 0))
        backward = [(target, source) for source, target in forward]
        low = lax.ppermute(
            lax.slice_in_dim(block, block.shape[dim] - width, None, axis=dim), axis, forward
        )
        high = lax.ppermute(lax.slice_in_dim(block, 0, width, axis=dim), axis, backward)
        block = jnp.concatenate([low, block, high], axis=dim)
    return block


def convolve(padded, weight, width_out):
    rows = padded.shape[1] - 2
    total = jnp.zeros((padded.shape[0], rows, weight.shape[2], width_out), jnp.float32)
    for a in range(3):
        for b in range(3):
            piece = padded[:, a : a + rows, :, b : b + width_out]
            total = total + jnp.einsum(
                "oc,vlcn->vlon", weight[a, b], piece, preferred_element_type=jnp.float32
            )
    return total


def pad_rows(field):
    return jnp.pad(field, ((0, 0), (1, 1), (0, 0), (0, 0)))


def exclusive_sum(values):
    running = jnp.cumsum(values, axis=0)
    return jnp.concatenate([jnp.zeros_like(values[:1]), running[:-1]], axis=0)


def body(window, anchor, noise, conv_in, conv_out, time_shift, plan, start):
    levels_here = window.shape[0]
    width = window.shape[3]
    offset = start[0] + lax.axis_index("lvl") * levels_here
    times = lax.dynamic_slice(plan, (offset,), (levels_here + 1,)).astype(jnp.float32)
    t_now = times[:-1]
    beta = 0.1 + 19.9 * t_now / 1000.0
    step = (t_now - times[1:]) / 1000.0
    beta_col = beta[:, None, None, None]
    step_col = step[:, None, None, None]
    spread = jnp.sqrt(beta * step)[:, None, None, None] * noise
    shift = (t_now / 1000.0)[:, None, None, None] * time_shift[None, None, :, None]
    states = window
    inclusive = None
    for sweep in range(SWEEPS):
        rounded = states.astype(jnp.bfloat16)
        wide = extended(rounded, (("lon", 3),), 2)
        pre = convolve(pad_rows(wide), conv_in, width + 2)
        hidden = jax.nn.silu(pre + shift).astype(jnp.bfloat16)
        score = convolve(pad_rows(hidden), conv_out, width)
        increment = (0.5 * beta_col * states + beta_col * score) * step_col + spread
        earlier = exclusive_sum(
            lax.all_to_all(increment, "lvl", split_axis=1, concat_axis=0, tiled=True)
        )
        before = lax.all_to_all(earlier, "lvl", split_axis=0, concat_axis=1, tiled=True)
        inclusive = before + increment
        states = anchor[None] + before
    return anchor[None] + inclusive


def solution(mesh):
    return jax.shard_map(
        body,
        mesh=mesh,
        in_specs=(
            P("lvl", None, None, "lon"),
            P(None, None, "lon"),
            P("lvl", None, None, "lon"),
            P(),
            P(),
            P(),
            P(),
            P(),
        ),
        out_specs=P("lvl", None, None, "lon"),
        check_vma=False,
    )
```

profile of v0, /device:TPU:1, one launch (start us, length us, event | category | flops | bytes accessed | tf_op | source)
XLA Modules:
  0.0 144.8 jit_solution(17149274946202437910)
XLA Ops:
  0.0 1.4 copy.128
  1.5 2.8 %collective-permute-start = (bf16[1,16,69,2]{2,3,1,0:T(2,128)(2,1)S(1)}, bf16[1,16,69,2]{2,3,1,0:T(2,128)(2,1)S(1)}, u32[]{:S(2)}, u32[]{:S(2)}) collective-permute-start(bf16[1,16,69,2]{2,3,1,0:T(2,128)(2,1)S(1)} %get-tuple-element.12), channel_id=1, source_target_pairs={{0,1},{1,2},{2,3},{3,4},{4,5},{5,6},{6,7},{7,8},{8,9},{9,10},{10,1... | collective-permute-start | bytes 13256 | tf_op jit(solution)/shard_map/ppermute | solution.py:15
  4.2 0.6 collective-permute-start.1
  5.5 0.8 dynamic-slice_convert_fusion
  6.3 0.6 fusion.220
  7.5 0.7 broadcast_multiply_fusion
  14.1 1.3 fusion.6
  19.5 0.8 fusion.92
  20.3 0.6 copy.147
  20.8 25.6 %all_to_all.48 = f32[1,16,69,128]{3,0,2,1:T(1,128)S(1)} all-to-all(f32[1,16,69,128]{3,0,2,1:T(1,128)S(1)} %copy.147), channel_id=1, replica_groups=mesh['lvl'=16,'lon'=16] {'lvl'}, dimensions={1} | all-to-all | bytes 1130496 | tf_op jit(solution)/shard_map/all_to_all | solution.py:66
  47.5 22.9 %all_to_all.49 = f32[16,1,69,128]{3,1,2,0:T(1,128)S(1)} all-to-all(f32[16,1,69,128]{3,1,2,0:T(1,128)S(1)} %concatenate.27.clone), channel_id=1, replica_groups=mesh['lvl'=16,'lon'=16] {'lvl'}, dimensions={0} | all-to-all | bytes 1130496 | tf_op jit(solution)/shard_map/all_to_all | solution.py:68
  70.7 5.7 %collective-permute-start.2 = (bf16[1,16,69,2]{3,1,2,0:T(8,128)(2,1)S(1)}, bf16[1,16,69,2]{3,1,2,0:T(8,128)(2,1)S(1)}, u32[]{:S(2)}, u32[]{:S(2)}) collective-permute-start(bf16[1,16,69,2]{3,1,2,0:T(8,128)(2,1)S(1)} %get-tuple-element.16), channel_id=1, source_target_pairs={{0,1},{1,2},{2,3},{3,4},{4,5},{5,6},{6,7},{7,8},{8,9},{9,10},{10,1... | collective-permute-start | bytes 13256 | tf_op jit(solution)/shard_map/ppermute | solution.py:15
  76.3 6.6 %collective-permute-done.2 = bf16[1,16,69,2]{3,1,2,0:T(8,128)(2,1)S(1)} collective-permute-done((bf16[1,16,69,2]{3,1,2,0:T(8,128)(2,1)S(1)}, bf16[1,16,69,2]{3,1,2,0:T(8,128)(2,1)S(1)}, u32[]{:S(2)}, u32[]{:S(2)}) %collective-permute-start.2) | collective-permute-done | bytes 4448 | tf_op jit(solution)/shard_map/ppermute | solution.py:15
  82.9 2.5 %collective-permute-done.3 = bf16[1,16,69,2]{3,1,2,0:T(8,128)(2,1)S(1)} collective-permute-done((bf16[1,16,69,2]{3,1,2,0:T(8,128)(2,1)S(1)}, bf16[1,16,69,2]{3,1,2,0:T(8,128)(2,1)S(1)}, u32[]{:S(2)}, u32[]{:S(2)}) %collective-permute-start.3) | collective-permute-done | bytes 4448 | tf_op jit(solution)/shard_map/ppermute | solution.py:18
  86.7 1.6 %fusion.84 = (bf16[16,69,130]{2,0,1:T(8,128)(2,1)S(1)}, bf16[16,69,130]{2,0,1:T(8,128)(2,1)S(1)}, bf16[16,69,130]{2,0,1:T(8,128)(2,1)S(1)}, bf16[16,69,130]{2,0,...) fusion(bf16[1,16,69,132]{3,1,2,0:T(8,128)(2,1)S(1)} %pad_maximu, ...), kind=kLoop, calls=%fused_computation.102 | loop fusion | bytes 3139776 | tf_op jit(solution)/shard_map/reshape.50
  88.3 0.6 fusion.77
  88.9 0.6 fusion.75
  89.5 0.6 fusion.68
  91.8 0.6 fusion.79
  92.4 1.5 %fusion.7 = bf16[1,16,192,130]{2,3,1,0:T(8,128)(2,1)S(1)} fusion(f32[16,130,192]{2,1,0:T(8,128)S(1)} %fusion.64, f32[16,130,192]{2,1,0:T(8,128)S(1)} %fusion.66, f32[16,130,192]{2,1,0:T(8,128)S(1)} %fusion.68, f32[16,130,192]{2,1,0:T(8,128)S(1)} %fusion.71, f32[16,130,192]{2,1,0:T(8,128)S(1)} %fusion.73, f32[16,130,192]{2,1,0:T(8,128)S(1)} %fusion.75, ...), kind=kOutput, calls=%fused_computation.13 | convolution fusion | flops 60702720 | bytes 19227648 | tf_op jit(solution)/shard_map/oc,vlcn->vlon/dot_general | solution.py:29
  97.9 0.8 fusion.90
  99.3 21.6 %all_to_all.50 = f32[1,16,69,128]{3,0,2,1:T(1,128)S(1)} all-to-all(f32[1,16,69,128]{3,0,2,1:T(1,128)S(1)} %copy.178), channel_id=1, replica_groups=mesh['lvl'=16,'lon'=16] {'lvl'}, dimensions={1} | all-to-all | bytes 1130496 | tf_op jit(solution)/shard_map/all_to_all | solution.py:66
  122.0 21.9 %all_to_all.51 = f32[16,1,69,128]{3,1,2,0:T(1,128)S(1)} all-to-all(f32[16,1,69,128]{3,1,2,0:T(1,128)S(1)} %concatenate.31.clone), channel_id=1, replica_groups=mesh['lvl'=16,'lon'=16] {'lvl'}, dimensions={0} | all-to-all | bytes 1130496 | tf_op jit(solution)/shard_map/all_to_all | solution.py:68
  143.9 0.9 fusion.93
  (58 shorter events, 17.6 us)
Async XLA Ops:
  0.0 10.5 %copy-start.3 = (bf16[3,3,192,69]{2,3,1,0:T(8,128)(2,1)S(1)}, bf16[3,3,192,69]{2,3,1,0:T(8,128)(2,1)}, u32[]{:S(2)}) copy-start(bf16[3,3,192,69]{2,3,1,0:T(8,128)(2,1)} %param.11) | copy-start | bytes 715396
  1.5 8.8 %collective-permute-start = (bf16[1,16,69,2]{2,3,1,0:T(2,128)(2,1)S(1)}, bf16[1,16,69,2]{2,3,1,0:T(2,128)(2,1)S(1)}, u32[]{:S(2)}, u32[]{:S(2)}) collective-permute-start(bf16[1,16,69,2]{2,3,1,0:T(2,128)(2,1)S(1)} %get-tuple-element.12), channel_id=1, source_target_pairs={{0,1},{1,2},{2,3},{3,4},{4,5},{5,6},{6,7},{7,8},{8,9},{9,10},{10,1... | collective-permute-start | bytes 13256 | tf_op jit(solution)/shard_map/ppermute | solution.py:15
  4.2 6.1 %collective-permute-start.1 = (bf16[1,16,69,2]{2,3,1,0:T(2,128)(2,1)S(1)}, bf16[1,16,69,2]{2,3,1,0:T(2,128)(2,1)S(1)}, u32[]{:S(2)}, u32[]{:S(2)}) collective-permute-start(bf16[1,16,69,2]{2,3,1,0:T(2,128)(2,1)S(1)} %get-tuple-element.13), channel_id=1, source_target_pairs={{1,0},{2,1},{3,2},{4,3},{5,4},{6,5},{7,6},{8,7},{9,8},{10,9},{11,1... | collective-permute-start | bytes 13256 | tf_op jit(solution)/shard_map/ppermute | solution.py:18
  14.1 1.4 copy-start.4
  18.1 1.4 copy-start.1
  18.1 1.4 copy-start.2
  46.5 23.9 %copy-start = (f32[16,69,128]{2,0,1:T(8,128)S(1)}, f32[16,69,128]{2,0,1:T(8,128)}, u32[]{:S(2)}) copy-start(f32[16,69,128]{2,0,1:T(8,128)} %param.9) | copy-start | bytes 1695748
  70.7 12.2 %collective-permute-start.2 = (bf16[1,16,69,2]{3,1,2,0:T(8,128)(2,1)S(1)}, bf16[1,16,69,2]{3,1,2,0:T(8,128)(2,1)S(1)}, u32[]{:S(2)}, u32[]{:S(2)}) collective-permute-start(bf16[1,16,69,2]{3,1,2,0:T(8,128)(2,1)S(1)} %get-tuple-element.16), channel_id=1, source_target_pairs={{0,1},{1,2},{2,3},{3,4},{4,5},{5,6},{6,7},{7,8},{8,9},{9,10},{10,1... | collective-permute-start | bytes 13256 | tf_op jit(solution)/shard_map/ppermute | solution.py:15
  76.3 9.0 %collective-permute-start.3 = (bf16[1,16,69,2]{3,1,2,0:T(8,128)(2,1)S(1)}, bf16[1,16,69,2]{3,1,2,0:T(8,128)(2,1)S(1)}, u32[]{:S(2)}, u32[]{:S(2)}) collective-permute-start(bf16[1,16,69,2]{3,1,2,0:T(8,128)(2,1)S(1)} %get-tuple-element.17), channel_id=1, source_target_pairs={{1,0},{2,1},{3,2},{4,3},{5,4},{6,5},{7,6},{8,7},{9,8},{10,9},{11,1... | collective-permute-start | bytes 13256 | tf_op jit(solution)/shard_map/ppermute | solution.py:18
where the time goes:
time: 145 us
  blocking collectives  92.1 us (64%)
  matrix products  19 us (13%)
  waiting for transfers between devices  9.05 us (6%)
  starting transfers between devices  9.03 us (6%)
  local copies, waits for them, and re-layouts  6.92 us (5%)
  other arithmetic  5.08 us (4%)
  between operations  3.68 us (3%)
    all_to_all x2, blocking collectives, body(): lax.all_to_all(increment, 'lvl', split_axis=1, concat_axis=0, tiled=True)  47.2 us
    all_to_all x2, blocking collectives, body(): lax.all_to_all(earlier, 'lvl', split_axis=0, concat_axis=1, tiled=True)  44.8 us
    dot_general x36, matrix products, convolve(): jnp.einsum('oc,vlcn->vlon', weight[a, b], piece, preferred_element_type=j...  19 us
    ppermute x2, starting transfers between devices, extended(): lax.ppermute(lax.slice_in_dim(block, block.shape[dim] - width, None, axis...  8.41 us
    ppermute x2, waiting for transfers between devices, extended(): lax.ppermute(lax.slice_in_dim(block, block.shape[dim] - width, None, axis...  6.56 us
  transfers between devices with their start and end apart: 4, of which 2 were waited for; matrix products, arithmetic and copies ran while one was open for 1% of the time, Pallas kernels for 0%

commit v1 on v0

v1 whole, which is shorter than its diff:
```python
import functools

import jax
import jax.numpy as jnp
from jax import lax
from jax.experimental import pallas as pl
from jax.experimental.pallas import tpu as pltpu
from jax.sharding import PartitionSpec as P

MESH = pl.DeviceIdType.MESH
F32 = jnp.float32
BF16 = jnp.bfloat16

RING = 8
HOP = 3
CROSS = 4
HALO = 3


def kernel(
    window, anchor, noise, conv_in, conv_out, time_shift, plan, start, out,
    xb, halo, xs, hid, w1, w2, coef, shift, state, inc,
    pin, pout, sin, sout, tin, tout,
    hsend, hrecv, psend, precv, ssend, srecv, tsend, trecv,
):
    lats, cin, width = window.shape
    hidden = time_shift.shape[1]
    step_c = 80
    last = RING - 1
    lvl = lax.axis_index("lvl")
    lon = lax.axis_index("lon")
    nlon = lax.axis_size("lon")
    ring = lvl // RING
    z = lvl % RING
    right = lax.rem(lon + 1, nlon)
    left = lax.rem(lon + nlon - 1, nlon)
    base = ring * RING
    above = base + lax.rem(z + 1, RING)
    below = base + lax.rem(z + RING - 1, RING)
    other = (1 - ring) * RING + z

    barrier = pltpu.get_barrier_semaphore()
    for target in ((lvl, left), (lvl, right), (above, lon), (below, lon), (other, lon)):
        pl.semaphore_signal(barrier, inc=1, device_id=target, device_id_type=MESH)

    t_now = plan[start[0] + lvl]
    t_next = plan[start[0] + lvl + 1]
    tv = jnp.full((8, width), t_now.astype(F32))
    uv = jnp.full((8, width), t_next.astype(F32))
    beta = 0.1 + 19.9 * tv / 1000.0
    dt = (tv - uv) / 1000.0
    coef[0] = beta
    coef[1] = dt
    coef[2] = jnp.sqrt(beta * dt)
    rows = lax.broadcasted_iota(jnp.int32, (hidden, hidden), 0)
    cols = lax.broadcasted_iota(jnp.int32, (hidden, hidden), 1)
    spread = jnp.where(rows == cols, jnp.broadcast_to(time_shift[...], (hidden, hidden)), 0.0)
    column = jnp.sum(spread, axis=1, keepdims=True)
    shift[...] = jnp.broadcast_to(column, (hidden, width)) * (tv[0:1, :] / 1000.0)
    w1[...] = jnp.zeros_like(w1)
    w2[...] = jnp.zeros_like(w2)
    for a in range(3):
        for b in range(3):
            w1[a, :, b * step_c : b * step_c + cin] = conv_in[a, b]
            w2[a, b * step_c : b * step_c + cin, :] = conv_out[a, b]
    xs[...] = jnp.zeros_like(xs)
    hid[...] = jnp.zeros_like(hid)

    @pl.when(z == 0)
    def _():
        pin[...] = jnp.zeros_like(pin)

    @pl.when(z == last)
    def _():
        sin[...] = jnp.zeros_like(sin)

    @pl.when(ring == 0)
    def _():
        tin[...] = jnp.zeros_like(tin)

    pl.semaphore_wait(barrier, 5)

    def halo_copy(s, side, l):
        target = right if side == 0 else left
        return pltpu.make_async_remote_copy(
            src_ref=xb.at[s, l], dst_ref=halo.at[s, side, l],
            send_sem=hsend.at[s, side, l], recv_sem=hrecv.at[s, side, l],
            device_id=(lvl, target), device_id_type=MESH,
        )

    def chain_copy(src, dst, send, recv, target, s, l):
        return pltpu.make_async_remote_copy(
            src_ref=src.at[s, l], dst_ref=dst.at[s, l],
            send_sem=send.at[s, l], recv_sem=recv.at[s, l],
            device_id=(target, lon), device_id_type=MESH,
        )

    def p_copy(s, l):
        return chain_copy(pout, pin, psend, precv, above, s, l)

    def s_copy(s, l):
        return chain_copy(sout, sin, ssend, srecv, below, s, l)

    def t_copy(s, l):
        return chain_copy(tout, tin, tsend, trecv, other, s, l)

    def first(l, carry):
        xb[0, l] = window[l].astype(BF16)
        halo_copy(0, 0, l).start()
        halo_copy(0, 1, l).start()
        return carry

    lax.fori_loop(0, lats, first, 0)

    lane = lax.broadcasted_iota(jnp.int32, (cin, width), 1)

    def place(s, l):
        halo_copy(s, 0, l).wait_recv()
        halo_copy(s, 1, l).wait_recv()
        main = xb[s, l].astype(F32)
        from_left = halo[s, 0, l].astype(F32)
        from_right = halo[s, 1, l].astype(F32)
        edge = jnp.where(lane < width // 2, from_right, from_left)
        up = pltpu.roll(main, 1, axis=1)
        down = pltpu.roll(main, width - 1, axis=1)
        edge_up = pltpu.roll(edge, 1, axis=1)
        edge_down = pltpu.roll(edge, width - 1, axis=1)
        low = lane == 0
        high = lane == width - 1
        xs[s, l + 1, 0:cin, 0:width] = jnp.where(low, edge_up, up).astype(BF16)
        xs[s, l + 1, 0:cin, width:] = jnp.where(low, up, edge_up).astype(BF16)
        xs[s, l + 1, step_c : step_c + cin, 0:width] = main.astype(BF16)
        xs[s, l + 1, step_c : step_c + cin, width:] = edge.astype(BF16)
        xs[s, l + 1, 2 * step_c : 2 * step_c + cin, 0:width] = jnp.where(high, edge_down, down).astype(BF16)
        xs[s, l + 1, 2 * step_c : 2 * step_c + cin, width:] = jnp.where(high, down, edge_down).astype(BF16)

    def activate(s, l):
        total = jnp.dot(w1[0], xs[s, l], preferred_element_type=F32)
        total += jnp.dot(w1[1], xs[s, l + 1], preferred_element_type=F32)
        total += jnp.dot(w1[2], xs[s, l + 2], preferred_element_type=F32)
        offset = shift[...]
        v = total + jnp.concatenate([offset, offset], axis=1)
        hid[s, l + 1] = (v / (1.0 + jnp.exp(-v))).astype(BF16)

    lane8 = lax.broadcasted_iota(jnp.int32, (step_c, width), 1)

    def advance(s, l, current):
        total = jnp.dot(w2[0], hid[s, l], preferred_element_type=F32)
        total += jnp.dot(w2[1], hid[s, l + 1], preferred_element_type=F32)
        total += jnp.dot(w2[2], hid[s, l + 2], preferred_element_type=F32)
        before = total[0:step_c]
        middle = total[step_c : 2 * step_c]
        after = total[2 * step_c : 3 * step_c]
        a0 = pltpu.roll(before[:, 0:width], 1, axis=1)
        a1 = pltpu.roll(before[:, width:], 1, axis=1)
        c0 = pltpu.roll(after[:, 0:width], width - 1, axis=1)
        c1 = pltpu.roll(after[:, width:], width - 1, axis=1)
        score = jnp.where(lane8 == 0, a1, a0) + middle[:, 0:width] + jnp.where(lane8 == width - 1, c1, c0)
        score = score[0:cin]
        bv, dv, nv = coef[0, 0:1], coef[1, 0:1], coef[2, 0:1]
        inc[s, l] = (0.5 * bv * current + bv * score) * dv + nv * noise[l]

    def inside(l):
        return jnp.logical_and(l >= 0, l < lats)

    def chain_p(s, l):
        @pl.when(z > 0)
        def _():
            p_copy(s, l).wait_recv()

        @pl.when(z < last)
        def _():
            pout[s, l] = pin[s, l] + inc[s, l]
            p_copy(s, l).start()

    def chain_s(s, l):
        @pl.when(z < last)
        def _():
            s_copy(s, l).wait_recv()

        sout[s, l] = sin[s, l] + inc[s, l]

        @pl.when(z > 0)
        def _():
            s_copy(s, l).start()

    far = jnp.maximum(z, last - z)
    ready = jnp.where(ring == 0, HOP * z, HOP * far + CROSS)
    second_p = jnp.where(ring == 0, HOP * z, HOP * last + CROSS + HOP * z)
    second_s = HOP * last + HOP * (last - z)
    finish = jnp.where(ring == 0, HOP * z, HOP * last + CROSS + HOP * far)
    begin2 = 4 + HALO
    steps = lats + begin2 + HOP * last + CROSS + HOP * last

    def step(t, carry):
        @pl.when(t < lats)
        def _():
            place(0, t)

        @pl.when(inside(t - 1))
        def _():
            activate(0, t - 1)

        @pl.when(inside(t - 2))
        def _():
            advance(0, t - 2, window[t - 2])

        lp = t - 2 - HOP * z

        @pl.when(inside(lp))
        def _():
            chain_p(0, lp)

        @pl.when(ring == 0)
        def _():
            ls = t - 2 - HOP * (last - z)

            @pl.when(inside(ls))
            def _():
                chain_s(0, ls)

            lt = t - 2 - HOP * far

            @pl.when(inside(lt))
            def _():
                tout[0, lt] = pin[0, lt] + sout[0, lt]
                t_copy(0, lt).start()

        le = t - 2 - ready

        @pl.when(inside(le))
        def _():
            @pl.when(ring == 1)
            def _():
                t_copy(0, le).wait_recv()

            x = anchor[le] + (pin[0, le] + tin[0, le])
            state[le] = x
            xb[1, le] = x.astype(BF16)
            halo_copy(1, 0, le).start()
            halo_copy(1, 1, le).start()

        lx = le - HALO

        @pl.when(inside(lx))
        def _():
            place(1, lx)

        @pl.when(inside(lx - 1))
        def _():
            activate(1, lx - 1)

        @pl.when(inside(lx - 2))
        def _():
            advance(1, lx - 2, state[lx - 2])

        lq = t - begin2 - second_p

        @pl.when(inside(lq))
        def _():
            chain_p(1, lq)

        @pl.when(ring == 0)
        def _():
            lr = t - begin2 - second_s

            @pl.when(inside(lr))
            def _():
                chain_s(1, lr)
                tout[1, lr] = pin[1, lr] + sout[1, lr]
                t_copy(1, lr).start()

        lf = t - begin2 - finish

        @pl.when(inside(lf))
        def _():
            @pl.when(ring == 1)
            def _():
                t_copy(1, lf).wait_recv()

            out[lf] = anchor[lf] + (pin[1, lf] + tin[1, lf] + inc[1, lf])

        return carry

    lax.fori_loop(0, steps, step, 0)

    def drain(l, carry):
        for s in range(2):
            halo_copy(s, 0, l).wait_send()
            halo_copy(s, 1, l).wait_send()

            @pl.when(z < last)
            def _():
                p_copy(s, l).wait_send()

            @pl.when(ring == 0)
            def _():
                t_copy(s, l).wait_send()

                @pl.when(z > 0)
                def _():
                    s_copy(s, l).wait_send()

        return carry

    lax.fori_loop(0, lats, drain, 0)


def body(window, anchor, noise, conv_in, conv_out, time_shift, plan, start):
    _, lats, cin, width = window.shape
    hidden = time_shift.shape[0]
    vmem = pl.BlockSpec(memory_space=pltpu.VMEM)
    smem = pl.BlockSpec(memory_space=pltpu.SMEM)
    rows = (2, lats, cin, width)
    dma = pltpu.SemaphoreType.DMA
    out = pl.pallas_call(
        kernel,
        out_shape=jax.ShapeDtypeStruct((lats, cin, width), F32),
        in_specs=[vmem] * 6 + [smem] * 2,
        out_specs=vmem,
        scratch_shapes=[
            pltpu.VMEM(rows, BF16),
            pltpu.VMEM((2,) + rows, BF16),
            pltpu.VMEM((2, lats + 2, 256, 2 * width), BF16),
            pltpu.VMEM((2, lats + 2, hidden, 2 * width), BF16),
            pltpu.VMEM((3, hidden, 256), BF16),
            pltpu.VMEM((3, 240, hidden), BF16),
            pltpu.VMEM((3, 8, width), F32),
            pltpu.VMEM((hidden, width), F32),
            pltpu.VMEM((lats, cin, width), F32),
            pltpu.VMEM(rows, F32),
        ]
        + [pltpu.VMEM(rows, F32)] * 6
        + [dma((2, 2, lats))] * 2
        + [dma((2, lats))] * 6,
        compiler_params=pltpu.CompilerParams(
            collective_id=0, has_side_effects=True, vmem_limit_bytes=56 * 1024 * 1024
        ),
    )(window[0], anchor, noise[0], conv_in, conv_out, time_shift[None, :], plan, start)
    return out[None]


def solution(mesh):
    return jax.shard_map(
        body,
        mesh=mesh,
        in_specs=(
            P("lvl", None, None, "lon"),
            P(None, None, "lon"),
            P("lvl", None, None, "lon"),
            P(),
            P(),
            P(),
            P(),
            P(),
        ),
        out_specs=P("lvl", None, None, "lon"),
        check_vma=False,
    )
```

time: 145 us -> 101 us (0.70)
  the two profiles are of different devices: /device:TPU:1 before, /device:TPU:30 now
where the time goes in v1:
time: 101 us
  Pallas kernels  93.5 us (93%)
  local copies, waits for them, and re-layouts  6.77 us (7%)
    pallas_call x1, Pallas kernels, body(): pl.pallas_call(kernel, out_shape=jax.ShapeDtypeStruct((lats, cin, width),...  93.5 us
    unnamed x8, local copies, waits for them, and re-layouts  3.42 us

profile of v1, /device:TPU:30, one launch (start us, length us, event | category | flops | bytes accessed | tf_op | source)
XLA Modules:
  0.0 101.0 jit_solution(4197241616618061573)
XLA Ops:
  0.0 0.0 copy-start
  0.7 2.0 %copy.12.conv_in = bf16[3,3,192,69]{3,2,1,0:T(8,128)(2,1)} copy(bf16[3,3,192,69]{2,3,1,0:T(8,128)(2,1)} %param.11) | data formatting | bytes 476928 | tf_op args[3]
  2.7 0.0 copy-done
  2.7 0.0 copy-start.1
  2.7 0.0 copy-start.2
  2.7 1.0 %copy.11.anchor = f32[16,69,128]{2,1,0:T(8,128)} copy(f32[16,69,128]{2,0,1:T(8,128)S(1)} %copy-done) | data formatting | bytes 1130496 | tf_op args[1]
  3.7 0.0 copy-done.1
  3.8 0.4 copy-done.2
  4.1 1.4 %copy_bitcast_fusion = (f32[16,69,128]{2,1,0:T(8,128)}, f32[16,69,128]{2,1,0:T(8,128)}) fusion(f32[1,16,69,128]{3,1,2,0:T(8,128)S(1)} %copy-done.1, f32[1,16,69,128]{3,1,2,0:T(8,128)S(1)} %copy-done.2), kind=kLoop, calls=%fused_computation | loop fusion | bytes 2260992 | tf_op jit(solution)/shard_map/squeeze | solution.py:339
  5.5 93.5 %shard_map.82 = f32[16,69,128]{2,1,0:T(8,128)} custom-call(f32[16,69,128]{2,1,0:T(8,128)} %get-tuple-element.6.window, f32[16,69,128]{2,1,0:T(8,128)} %copy.11.anchor, f32[16,69,128]{2,1,0:T(8,128)} %get-tuple-element.5.noise, bf16[3,3,192,69]{3,2,1,0:T(8,128)(2,1)} %copy.12.conv_in, bf16[3,3,69,192]{3,2,1,0:T(8,128)(2,1)} %conv_out.1, f32[1,192]{1,0:T(1,128)} %bitcast.7, ...), custom_call_target="tpu_custom_call" | custom-call | tf_op jit(solution)/shard_map/pallas_call | solution.py:316
  99.0 2.0 %copy.13 = f32[1,16,69,128]{3,1,2,0:T(8,128)} copy(f32[1,16,69,128]{3,2,1,0:T(8,128)} %bitcast.6) | data formatting | bytes 1130496 | tf_op jit(solution)/shard_map/broadcast_in_dim | solution.py:340
Async XLA Ops:
  0.0 2.7 %copy-start = (f32[16,69,128]{2,0,1:T(8,128)S(1)}, f32[16,69,128]{2,0,1:T(8,128)}, u32[]{:S(2)}) copy-start(f32[16,69,128]{2,0,1:T(8,128)} %param.9) | copy-start | bytes 1695748
  2.7 1.1 %copy-start.1 = (f32[1,16,69,128]{3,1,2,0:T(8,128)S(1)}, f32[1,16,69,128]{3,1,2,0:T(8,128)}, u32[]{:S(2)}) copy-start(f32[1,16,69,128]{3,1,2,0:T(8,128)} %param.10) | copy-start | bytes 1695748
  2.7 1.4 %copy-start.2 = (f32[1,16,69,128]{3,1,2,0:T(8,128)S(1)}, f32[1,16,69,128]{3,1,2,0:T(8,128)}, u32[]{:S(2)}) copy-start(f32[1,16,69,128]{3,1,2,0:T(8,128)} %param.8) | copy-start | bytes 1695748

commit v2 on v1

--- a/solution.py
+++ b/solution.py
@@ -19,14 +19,15 @@
 
 def kernel(
     window, anchor, noise, conv_in, conv_out, time_shift, plan, start, out,
-    xb, halo, xs, hid, w1, w2, coef, shift, state, inc,
+    xb, halo, xs, hid, w1, w2, wt, coef, shift, state, inc,
     pin, pout, sin, sout, tin, tout,
-    hsend, hrecv, psend, precv, ssend, srecv, tsend, trecv,
+    hsend, hrecv, psend, precv, ssend, srecv, tsend, trecv, usend,
 ):
-    lats, cin, width = window.shape
+    lats, cin, width = state.shape
     hidden = time_shift.shape[1]
     step_c = 80
     last = RING - 1
+    half = RING // 2
     lvl = lax.axis_index("lvl")
     lon = lax.axis_index("lon")
     nlon = lax.axis_size("lon")
@@ -42,6 +43,62 @@
     barrier = pltpu.get_barrier_semaphore()
     for target in ((lvl, left), (lvl, right), (above, lon), (below, lon), (other, lon)):
         pl.semaphore_signal(barrier, inc=1, device_id=target, device_id_type=MESH)
+
+    def row(l):
+        return pl.ds(l, cin, stride=lats)
+
+    def convert(l, carry):
+        xb[0, l] = window[row(l), :].astype(BF16)
+        return carry
+
+    lax.fori_loop(0, lats, convert, 0)
+
+    pl.semaphore_wait(barrier, 5)
+
+    def halo_copy(s, side, l):
+        target = right if side == 0 else left
+        return pltpu.make_async_remote_copy(
+            src_ref=xb.at[s, l], dst_ref=halo.at[s, side, l],
+            send_sem=hsend.at[s, side, l], recv_sem=hrecv.at[s, side, l],
+            device_id=(lvl, target), device_id_type=MESH,
+        )
+
+    def chain_copy(src, dst, send, recv, target, s, l):
+        return pltpu.make_async_remote_copy(
+            src_ref=src.at[s, l], dst_ref=dst.at[s, l],
+            send_sem=send.at[s, l], recv_sem=recv.at[s, l],
+            device_id=(target, lon), device_id_type=MESH,
+        )
+
+    def p_copy(s, l):
+        return chain_copy(pout, pin, psend, precv, above, s, l)
+
+    def s_copy(s, l):
+        return chain_copy(sout, sin, ssend, srecv, below, s, l)
+
+    def t_copy(s, l):
+        return chain_copy(tout if s == 0 else sout, tin, tsend, trecv, other, s, l)
+
+    def u_copy(l):
+        return pltpu.make_async_remote_copy(
+            src_ref=sout.at[1, l], dst_ref=sin.at[1, l],
+            send_sem=usend.at[l], recv_sem=srecv.at[1, l],
+            device_id=(above, lon), device_id_type=MESH,
+        )
+
+    def spread_copy(l):
+        return chain_copy(sin, tin, tsend, trecv, other, 1, l)
+
+    def relay_copy(l):
+        onward = jnp.where(jnp.logical_and(ring == 0, z < half - 1), above, below)
+        return chain_copy(sin, sin, ssend, srecv, onward, 1, l)
+
+    def first(l, carry):
+        halo_copy(0, 0, l).start()
+        halo_copy(0, 1, l).start()
+        return carry
+
+    lax.fori_loop(0, lats, first, 0)
 
     t_now = plan[start[0] + lvl]
     t_next = plan[start[0] + lvl + 1]
@@ -57,20 +114,38 @@
     spread = jnp.where(rows == cols, jnp.broadcast_to(time_shift[...], (hidden, hidden)), 0.0)
     column = jnp.sum(spread, axis=1, keepdims=True)
     shift[...] = jnp.broadcast_to(column, (hidden, width)) * (tv[0:1, :] / 1000.0)
-    w1[...] = jnp.zeros_like(w1)
+    wt[...] = jnp.zeros_like(wt)
     w2[...] = jnp.zeros_like(w2)
     for a in range(3):
         for b in range(3):
-            w1[a, :, b * step_c : b * step_c + cin] = conv_in[a, b]
+            wt[a, b * step_c : b * step_c + cin, :] = conv_in[a, b]
             w2[a, b * step_c : b * step_c + cin, :] = conv_out[a, b]
-    xs[...] = jnp.zeros_like(xs)
-    hid[...] = jnp.zeros_like(hid)
+    for a in range(3):
+        w1[a] = wt[a].T
+
+    blank = jnp.zeros((16, 2 * width), BF16)
+    for s in range(2):
+        for edge in (0, lats + 1):
+            xs[s, edge] = jnp.zeros((256, 2 * width), BF16)
+            hid[s, edge] = jnp.zeros((hidden, 2 * width), BF16)
+
+    def clear(l, carry):
+        for s in range(2):
+            for start_row in (64, 144, 224, 240):
+                xs[s, l + 1, start_row : start_row + 16] = blank
+        return carry
+
+    lax.fori_loop(0, lats, clear, 0)
 
     @pl.when(z == 0)
     def _():
         pin[...] = jnp.zeros_like(pin)
 
-    @pl.when(z == last)
+    @pl.when(jnp.logical_and(ring == 1, z == half))
+    def _():
+        pin[1] = jnp.zeros_like(pin[1])
+
+    @pl.when(z == jnp.where(ring == 0, last, half - 1))
     def _():
         sin[...] = jnp.zeros_like(sin)
 
@@ -78,39 +153,6 @@
     def _():
         tin[...] = jnp.zeros_like(tin)
 
-    pl.semaphore_wait(barrier, 5)
-
-    def halo_copy(s, side, l):
-        target = right if side == 0 else left
-        return pltpu.make_async_remote_copy(
-            src_ref=xb.at[s, l], dst_ref=halo.at[s, side, l],
-            send_sem=hsend.at[s, side, l], recv_sem=hrecv.at[s, side, l],
-            device_id=(lvl, target), device_id_type=MESH,
-        )
-
-    def chain_copy(src, dst, send, recv, target, s, l):
-        return pltpu.make_async_remote_copy(
-            src_ref=src.at[s, l], dst_ref=dst.at[s, l],
-            send_sem=send.at[s, l], recv_sem=recv.at[s, l],
-            device_id=(target, lon), device_id_type=MESH,
-        )
-
-    def p_copy(s, l):
-        return chain_copy(pout, pin, psend, precv, above, s, l)
-
-    def s_copy(s, l):
-        return chain_copy(sout, sin, ssend, srecv, below, s, l)
-
-    def t_copy(s, l):
-        return chain_copy(tout, tin, tsend, trecv, other, s, l)
-
-    def first(l, carry):
-        xb[0, l] = window[l].astype(BF16)
-        halo_copy(0, 0, l).start()
-        halo_copy(0, 1, l).start()
-        return carry
-
-    lax.fori_loop(0, lats, first, 0)
 
     lane = lax.broadcasted_iota(jnp.int32, (cin, width), 1)
 
@@ -140,7 +182,7 @@
         total += jnp.dot(w1[2], xs[s, l + 2], preferred_element_type=F32)
         offset = shift[...]
         v = total + jnp.concatenate([offset, offset], axis=1)
-        hid[s, l + 1] = (v / (1.0 + jnp.exp(-v))).astype(BF16)
+        hid[s, l + 1] = (0.5 * v * (1.0 + jnp.tanh(0.5 * v))).astype(BF16)
 
     lane8 = lax.broadcasted_iota(jnp.int32, (step_c, width), 1)
 
@@ -158,7 +200,7 @@
         score = jnp.where(lane8 == 0, a1, a0) + middle[:, 0:width] + jnp.where(lane8 == width - 1, c1, c0)
         score = score[0:cin]
         bv, dv, nv = coef[0, 0:1], coef[1, 0:1], coef[2, 0:1]
-        inc[s, l] = (0.5 * bv * current + bv * score) * dv + nv * noise[l]
+        inc[s, l] = (0.5 * bv * current + bv * score) * dv + nv * noise[row(l), :]
 
     def inside(l):
         return jnp.logical_and(l >= 0, l < lats)
@@ -186,11 +228,20 @@
 
     far = jnp.maximum(z, last - z)
     ready = jnp.where(ring == 0, HOP * z, HOP * far + CROSS)
-    second_p = jnp.where(ring == 0, HOP * z, HOP * last + CROSS + HOP * z)
-    second_s = HOP * last + HOP * (last - z)
-    finish = jnp.where(ring == 0, HOP * z, HOP * last + CROSS + HOP * far)
+    low = z < half
+    tail = HOP * last + CROSS
+    second_p = jnp.where(ring == 0, HOP * z, jnp.where(low, tail + HOP * z, ready))
+    away = jnp.where(z < half - 1, z + 1, last - z)
+    path = lax.rem(half - 1 - z + RING, RING)
+    reach = HOP * (last + away) + CROSS
+    trail = HOP * (half + path) + CROSS
+    second_s = jnp.where(ring == 0, HOP * (last + away), trail)
+    finish = jnp.where(ring == 0, HOP * z, jnp.maximum(reach, jnp.where(low, tail + HOP * z, trail)))
+    source = z == jnp.where(ring == 0, last, half - 1)
+    first_of_part = jnp.logical_or(z == 0, jnp.logical_and(ring == 1, z == half))
+    last_of_part = jnp.logical_or(z == last, jnp.logical_and(ring == 1, z == half - 1))
     begin2 = 4 + HALO
-    steps = lats + begin2 + HOP * last + CROSS + HOP * last
+    steps = lats + begin2 + HOP * (last + half) + CROSS
 
     def step(t, carry):
         @pl.when(t < lats)
@@ -203,7 +254,7 @@
 
         @pl.when(inside(t - 2))
         def _():
-            advance(0, t - 2, window[t - 2])
+            advance(0, t - 2, window[row(t - 2), :])
 
         lp = t - 2 - HOP * z
 
@@ -234,7 +285,7 @@
             def _():
                 t_copy(0, le).wait_recv()
 
-            x = anchor[le] + (pin[0, le] + tin[0, le])
+            x = anchor[row(le), :] + (pin[0, le] + tin[0, le])
             state[le] = x
             xb[1, le] = x.astype(BF16)
             halo_copy(1, 0, le).start()
@@ -258,17 +309,55 @@
 
         @pl.when(inside(lq))
         def _():
-            chain_p(1, lq)
-
-        @pl.when(ring == 0)
-        def _():
-            lr = t - begin2 - second_s
-
-            @pl.when(inside(lr))
-            def _():
-                chain_s(1, lr)
-                tout[1, lr] = pin[1, lr] + sout[1, lr]
-                t_copy(1, lr).start()
+            @pl.when(jnp.logical_not(first_of_part))
+            def _():
+                p_copy(1, lq).wait_recv()
+
+            @pl.when(jnp.logical_not(last_of_part))
+            def _():
+                pout[1, lq] = pin[1, lq] + inc[1, lq]
+                p_copy(1, lq).start()
+
+        lr = t - begin2 - second_s
+
+        @pl.when(inside(lr))
+        def _():
+            @pl.when(jnp.logical_not(source))
+            def _():
+                s_copy(1, lr).wait_recv()
+
+            @pl.when(ring == 0)
+            def _():
+                @pl.when(z == last)
+                def _():
+                    sout[1, lr] = pin[1, lr] + inc[1, lr]
+                    u_copy(lr).start()
+                    s_copy(1, lr).start()
+                    t_copy(1, lr).start()
+
+                @pl.when(z < last)
+                def _():
+                    spread_copy(lr).start()
+
+                @pl.when(jnp.logical_or(z < half - 2, jnp.logical_and(z >= half, z < last)))
+                def _():
+                    relay_copy(lr).start()
+
+            @pl.when(ring == 1)
+            def _():
+                @pl.when(z == half - 1)
+                def _():
+                    sout[1, lr] = inc[1, lr]
+                    s_copy(1, lr).start()
+
+                @pl.when(z < half - 1)
+                def _():
+                    sout[1, lr] = sin[1, lr] + inc[1, lr]
+                    s_copy(1, lr).start()
+
+                @pl.when(z > half)
+                def _():
+                    relay_copy(lr).start()
 
         lf = t - begin2 - finish
 
@@ -278,32 +367,61 @@
             def _():
                 t_copy(1, lf).wait_recv()
 
-            out[lf] = anchor[lf] + (pin[1, lf] + tin[1, lf] + inc[1, lf])
+            total = pin[1, lf] + tin[1, lf] + inc[1, lf]
+            upper = jnp.logical_and(ring == 1, z >= half)
+
+            @pl.when(upper)
+            def _():
+                out[row(lf), :] = anchor[row(lf), :] + (total + sin[1, lf])
+
+            @pl.when(jnp.logical_not(upper))
+            def _():
+                out[row(lf), :] = anchor[row(lf), :] + total
 
         return carry
 
     lax.fori_loop(0, steps, step, 0)
+
+    ends = jnp.logical_or(z == half - 1, z == half - 2)
+    passes = jnp.where(ring == 0, jnp.logical_not(ends), z != half)
 
     def drain(l, carry):
         for s in range(2):
             halo_copy(s, 0, l).wait_send()
             halo_copy(s, 1, l).wait_send()
 
-            @pl.when(z < last)
-            def _():
-                p_copy(s, l).wait_send()
-
             @pl.when(ring == 0)
             def _():
                 t_copy(s, l).wait_send()
 
-                @pl.when(z > 0)
-                def _():
-                    s_copy(s, l).wait_send()
+        @pl.when(z < last)
+        def _():
+            p_copy(0, l).wait_send()
+
+        @pl.when(jnp.logical_not(last_of_part))
+        def _():
+            p_copy(1, l).wait_send()
+
+        @pl.when(jnp.logical_and(ring == 0, z > 0))
+        def _():
+            s_copy(0, l).wait_send()
+
+        @pl.when(passes)
+        def _():
+            s_copy(1, l).wait_send()
+
+        @pl.when(jnp.logical_and(ring == 0, z == last))
+        def _():
+            u_copy(l).wait_send()
 
         return carry
 
     lax.fori_loop(0, lats, drain, 0)
+
+
+def rows_of(field):
+    lats, cin, width = field.shape
+    return field.transpose(1, 0, 2).reshape(cin * lats, width)
 
 
 def body(window, anchor, noise, conv_in, conv_out, time_shift, plan, start):
@@ -315,7 +433,7 @@
     dma = pltpu.SemaphoreType.DMA
     out = pl.pallas_call(
         kernel,
-        out_shape=jax.ShapeDtypeStruct((lats, cin, width), F32),
+        out_shape=jax.ShapeDtypeStruct((cin * lats, width), F32),
         in_specs=[vmem] * 6 + [smem] * 2,
         out_specs=vmem,
         scratch_shapes=[
@@ -325,6 +443,7 @@
             pltpu.VMEM((2, lats + 2, hidden, 2 * width), BF16),
             pltpu.VMEM((3, hidden, 256), BF16),
             pltpu.VMEM((3, 240, hidden), BF16),
+            pltpu.VMEM((3, 256, hidden), BF16),
             pltpu.VMEM((3, 8, width), F32),
             pltpu.VMEM((hidden, width), F32),
             pltpu.VMEM((lats, cin, width), F32),
@@ -332,12 +451,16 @@
         ]
         + [pltpu.VMEM(rows, F32)] * 6
         + [dma((2, 2, lats))] * 2
-        + [dma((2, lats))] * 6,
+        + [dma((2, lats))] * 6
+        + [dma((lats,))],
         compiler_params=pltpu.CompilerParams(
             collective_id=0, has_side_effects=True, vmem_limit_bytes=56 * 1024 * 1024
         ),
-    )(window[0], anchor, noise[0], conv_in, conv_out, time_shift[None, :], plan, start)
-    return out[None]
+    )(
+        rows_of(window[0]), rows_of(anchor), rows_of(noise[0]), conv_in.transpose(0, 1, 3, 2),
+        conv_out, time_shift[None, :], plan, start,
+    )
+    return out.reshape(cin, lats, width).transpose(1, 0, 2)[None]
 
 
 def solution(mesh):

time: 101 us -> 84.9 us (0.84)
  the two profiles are of different devices: /device:TPU:30 before, /device:TPU:126 now
where the time goes in v2:
time: 84.9 us; the launch traced here: 84.7 us
  Pallas kernels  82.2 us (97%)
  local copies, waits for them, and re-layouts  1.9 us (2%)
    pallas_call x1, Pallas kernels, body(): pl.pallas_call(kernel, out_shape=jax.ShapeDtypeStruct((cin * lats, width)...  82.2 us
    unnamed x1, local copies, waits for them, and re-layouts  1.9 us

profile of v2, /device:TPU:126, one launch (start us, length us, event | category | flops | bytes accessed | tf_op | source)
XLA Modules:
  0.0 84.7 jit_solution(11011254479436678682)
XLA Ops:
  0.7 82.2 %shard_map.82 = f32[1104,128]{1,0:T(8,128)} custom-call(f32[1104,128]{1,0:T(8,128)} %bitcast.21, f32[1104,128]{1,0:T(8,128)} %bitcast.22, f32[1104,128]{1,0:T(8,128)} %bitcast.23, bf16[3,3,69,192]{3,2,1,0:T(8,128)(2,1)} %bitcast.24, bf16[3,3,69,192]{3,2,1,0:T(8,128)(2,1)} %conv_out.1, f32[1,192]{1,0:T(1,128)} %bitcast.25, s32[256]{0:T(256)} %plan.1, ...), custom_call_target="tpu_custom_call" | custom-call | tf_op jit(solution)/shard_map/pallas_call | solution.py:434
  82.8 1.9 %copy.11 = f32[1,16,69,128]{3,1,2,0:T(8,128)} copy(f32[1,16,69,128]{3,1,2,0:T(8,128)} %bitcast.20) | data formatting | bytes 1130496

commit v3 on v2

--- a/solution.py
+++ b/solution.py
@@ -18,7 +18,8 @@
 
 
 def kernel(
-    window, anchor, noise, conv_in, conv_out, time_shift, plan, start, out,
+    window_hbm, anchor_hbm, noise_hbm, conv_in_hbm, conv_out_hbm, time_shift, plan, start, out,
+    window, anchor, noise, conv_in, conv_out, load_sem,
     xb, halo, xs, hid, w1, w2, wt, coef, shift, state, inc,
     pin, pout, sin, sout, tin, tout,
     hsend, hrecv, psend, precv, ssend, srecv, tsend, trecv, usend,
@@ -44,6 +45,16 @@
     for target in ((lvl, left), (lvl, right), (above, lon), (below, lon), (other, lon)):
         pl.semaphore_signal(barrier, inc=1, device_id=target, device_id_type=MESH)
 
+    loads = [
+        pltpu.make_async_copy(src, dst, load_sem.at[i])
+        for i, (src, dst) in enumerate((
+            (window_hbm, window), (conv_in_hbm, conv_in), (conv_out_hbm, conv_out),
+            (noise_hbm, noise), (anchor_hbm, anchor),
+        ))
+    ]
+    for load in loads:
+        load.start()
+
     def row(l):
         return pl.ds(l, cin, stride=lats)
 
@@ -51,6 +62,7 @@
         xb[0, l] = window[row(l), :].astype(BF16)
         return carry
 
+    loads[0].wait()
     lax.fori_loop(0, lats, convert, 0)
 
     pl.semaphore_wait(barrier, 5)
@@ -114,6 +126,8 @@
     spread = jnp.where(rows == cols, jnp.broadcast_to(time_shift[...], (hidden, hidden)), 0.0)
     column = jnp.sum(spread, axis=1, keepdims=True)
     shift[...] = jnp.broadcast_to(column, (hidden, width)) * (tv[0:1, :] / 1000.0)
+    for load in loads[1:]:
+        load.wait()
     wt[...] = jnp.zeros_like(wt)
     w2[...] = jnp.zeros_like(w2)
     for a in range(3):
@@ -240,7 +254,7 @@
     source = z == jnp.where(ring == 0, last, half - 1)
     first_of_part = jnp.logical_or(z == 0, jnp.logical_and(ring == 1, z == half))
     last_of_part = jnp.logical_or(z == last, jnp.logical_and(ring == 1, z == half - 1))
-    begin2 = 4 + HALO
+    begin2 = 6 + HALO
     steps = lats + begin2 + HOP * (last + half) + CROSS
 
     def step(t, carry):
@@ -248,15 +262,13 @@
         def _():
             place(0, t)
 
-        @pl.when(inside(t - 1))
-        def _():
-            activate(0, t - 1)
-
-        @pl.when(inside(t - 2))
-        def _():
-            advance(0, t - 2, window[row(t - 2), :])
-
-        lp = t - 2 - HOP * z
+        @pl.when(jnp.logical_and(t >= 1, t < lats + 3))
+        def _():
+            done = jnp.clip(t - 3, 0, lats - 1)
+            advance(0, done, window[row(done), :])
+            activate(0, jnp.minimum(t - 1, lats - 1))
+
+        lp = t - 3 - HOP * z
 
         @pl.when(inside(lp))
         def _():
@@ -264,20 +276,20 @@
 
         @pl.when(ring == 0)
         def _():
-            ls = t - 2 - HOP * (last - z)
+            ls = t - 3 - HOP * (last - z)
 
             @pl.when(inside(ls))
             def _():
                 chain_s(0, ls)
 
-            lt = t - 2 - HOP * far
+            lt = t - 3 - HOP * far
 
             @pl.when(inside(lt))
             def _():
                 tout[0, lt] = pin[0, lt] + sout[0, lt]
                 t_copy(0, lt).start()
 
-        le = t - 2 - ready
+        le = t - 3 - ready
 
         @pl.when(inside(le))
         def _():
@@ -297,13 +309,11 @@
         def _():
             place(1, lx)
 
-        @pl.when(inside(lx - 1))
-        def _():
-            activate(1, lx - 1)
-
-        @pl.when(inside(lx - 2))
-        def _():
-            advance(1, lx - 2, state[lx - 2])
+        @pl.when(jnp.logical_and(lx >= 1, lx < lats + 3))
+        def _():
+            done = jnp.clip(lx - 3, 0, lats - 1)
+            advance(1, done, state[done])
+            activate(1, jnp.minimum(lx - 1, lats - 1))
 
         lq = t - begin2 - second_p
 
@@ -429,14 +439,19 @@
     hidden = time_shift.shape[0]
     vmem = pl.BlockSpec(memory_space=pltpu.VMEM)
     smem = pl.BlockSpec(memory_space=pltpu.SMEM)
+    hbm = pl.BlockSpec(memory_space=pl.ANY)
     rows = (2, lats, cin, width)
     dma = pltpu.SemaphoreType.DMA
     out = pl.pallas_call(
         kernel,
         out_shape=jax.ShapeDtypeStruct((cin * lats, width), F32),
-        in_specs=[vmem] * 6 + [smem] * 2,
+        in_specs=[hbm] * 5 + [vmem] + [smem] * 2,
         out_specs=vmem,
-        scratch_shapes=[
+        scratch_shapes=[pltpu.VMEM((cin * lats, width), F32)] * 3
+        + [
+            pltpu.VMEM((3, 3, cin, hidden), BF16),
+            pltpu.VMEM((3, 3, cin, hidden), BF16),
+            dma((5,)),
             pltpu.VMEM(rows, BF16),
             pltpu.VMEM((2,) + rows, BF16),
             pltpu.VMEM((2, lats + 2, 256, 2 * width), BF16),

time: 84.9 us -> 83.8 us (0.987)
  Pallas kernels: 82.2 us -> 81 us
    pallas_call x1, Pallas kernels: 82.2 us -> 81 us  [body(): pl.pallas_call(kernel, out_shape=jax.ShapeDtypeStruct((cin * lats, width)...]
where the time goes in v3:
time: 83.8 us; the launch traced here: 83.6 us
  Pallas kernels  81 us (97%)
  local copies, waits for them, and re-layouts  1.9 us (2%)
    pallas_call x1, Pallas kernels, body(): pl.pallas_call(kernel, out_shape=jax.ShapeDtypeStruct((cin * lats, width)...  81 us
    unnamed x1, local copies, waits for them, and re-layouts  1.9 us

profile of v3, /device:TPU:126, one launch (start us, length us, event | category | flops | bytes accessed | tf_op | source)
XLA Modules:
  0.0 83.6 jit_solution(12941707762543674444)
XLA Ops:
  0.7 81.0 %shard_map.82 = f32[1104,128]{1,0:T(8,128)} custom-call(f32[1104,128]{1,0:T(8,128)} %bitcast.21, f32[1104,128]{1,0:T(8,128)} %bitcast.22, f32[1104,128]{1,0:T(8,128)} %bitcast.23, bf16[3,3,69,192]{3,2,1,0:T(8,128)(2,1)} %bitcast.24, bf16[3,3,69,192]{3,2,1,0:T(8,128)(2,1)} %conv_out_hbm.1, f32[1,192]{1,0:T(1,128)} %bitcast.25, s32[256]{0:T(256)} %plan.1, ...), custom_call_target="tpu_custom_call" | custom-call | tf_op jit(solution)/shard_map/pallas_call | solution.py:445
  81.7 1.9 %copy.11 = f32[1,16,69,128]{3,1,2,0:T(8,128)} copy(f32[1,16,69,128]{3,1,2,0:T(8,128)} %bitcast.20) | data formatting | bytes 1130496
